TPU v7x, 64 devices: a 2x2x8 block of a 4x4x8 slice. The times are simulated.
64 devices in a mesh: data: 4 (over x, y), seq: 16 (over z, core).
Axes of the slice: x: 2, y: 2, z: 8, core: 2. Of those that a mesh axis runs over, the one named last changes fastest.
The devices are a block of a 4x4x8 slice.
Arguments:
- x_tok: bfloat16 [131072, 1024], P(('data', 'seq')), parts along dimension 0
- dy_tok: bfloat16 [131072, 1024], P(('data', 'seq')), parts along dimension 0
- ln_gamma: float32 [1024], replicated
- ln_beta: float32 [1024], replicated
- w_qkv: bfloat16 [1024, 3, 16, 64], replicated
- w_out: bfloat16 [1024, 1024], replicated
Outputs:
- output 1: bfloat16 [131072, 1024], P(('data', 'seq')), parts along dimension 0
- output 2: bfloat16 [131072, 1024], P(('data', 'seq')), parts along dimension 0
- output 3: float32 [4096, 3, 16, 64], P(('data', 'seq')), parts along dimension 0
- output 4: float32 [4096, 1024], P(('data', 'seq')), parts along dimension 0
- output 5: float32 [4096], P('data'), parts along dimension 0
- output 6: float32 [4096], P('data'), parts along dimension 0
There are 4 independent parts. A program takes and returns all parts, laid end to end along the dimension named above; an argument that names none is the same for every part.
All inputs are finite; a program needn't handle non-finite values.
Results may differ from a plain program's by a relative error of at most 0.00487299.
Values are sent between devices in bfloat16 or wider.
A program may use at most 768 MiB of HBM per device.

v0:
```python
import jax
import jax.numpy as jnp
from jax import lax
from jax.sharding import PartitionSpec as P

LN_EPS = 1e-5


def phi_act(t):
    return jnp.where(t > 0, t + 1.0, jnp.exp(jnp.minimum(t, 0.0)))


def phi_slope(t):
    return jnp.where(t > 0, 1.0, jnp.exp(jnp.minimum(t, 0.0)))


def local_block(x_tok, dy_tok, ln_gamma, ln_beta, w_qkv, w_out):
    tokens, width = x_tok.shape
    heads = w_qkv.shape[2]
    head_dim = w_qkv.shape[3]
    x_f32 = x_tok.astype(jnp.float32)
    centered = x_f32 - jnp.mean(x_f32, axis=-1, keepdims=True)
    inv_std = lax.rsqrt(jnp.mean(centered * centered, axis=-1, keepdims=True) + LN_EPS)
    x_hat = centered * inv_std
    normed = (x_hat * ln_gamma + ln_beta).astype(jnp.bfloat16)
    w_flat = w_qkv.reshape(width, 3 * width)
    qkv_all = jnp.dot(normed, w_flat, preferred_element_type=jnp.float32).astype(jnp.bfloat16)
    qkv_all = qkv_all.reshape(tokens, 3, heads, head_dim)
    q_raw = qkv_all[:, 0].astype(jnp.float32)
    k_raw = qkv_all[:, 1].astype(jnp.float32)
    values = qkv_all[:, 2]
    feat_q = phi_act(q_raw).astype(jnp.bfloat16)
    feat_k = phi_act(k_raw).astype(jnp.bfloat16)
    state_part = jnp.einsum("nhi,nhj->hij", feat_k, values, preferred_element_type=jnp.float32)
    norm_part = jnp.sum(feat_k, axis=0, dtype=jnp.float32)
    state, norm_vec = lax.psum((state_part, norm_part), "seq")
    state_b = state.astype(jnp.bfloat16)
    norm_b = norm_vec.astype(jnp.bfloat16)
    numerator = jnp.einsum("nhi,hij->nhj", feat_q, state_b, preferred_element_type=jnp.float32)
    denominator = jnp.einsum("nhi,hi->nh", feat_q, norm_b, preferred_element_type=jnp.float32)
    att_f32 = numerator / denominator[:, :, None]
    att_out = att_f32.astype(jnp.bfloat16).reshape(tokens, width)
    y_tok = (x_f32 + jnp.dot(att_out, w_out, preferred_element_type=jnp.float32)).astype(jnp.bfloat16)
    dwout_part = jnp.einsum("nc,nd->cd", att_out, dy_tok, preferred_element_type=jnp.float32)
    dw_out = lax.psum_scatter(dwout_part, "seq", scatter_dimension=0, tiled=True)
    d_att = jnp.einsum("nd,cd->nc", dy_tok, w_out, preferred_element_type=jnp.float32).reshape(tokens, heads, head_dim)
    g_scaled = (d_att / denominator[:, :, None]).astype(jnp.bfloat16)
    correction = jnp.sum(g_scaled * att_f32, axis=-1)
    d_fq = jnp.einsum("nhj,hij->nhi", g_scaled, state_b, preferred_element_type=jnp.float32) - correction[:, :, None] * norm_b
    dstate_part = jnp.einsum("nhi,nhj->hij", feat_q, g_scaled, preferred_element_type=jnp.float32)
    dnorm_part = -jnp.sum(correction[:, :, None] * feat_q, axis=0)
    d_state, d_norm = lax.psum((dstate_part, dnorm_part), "seq")
    d_state_b = d_state.astype(jnp.bfloat16)
    d_fk = jnp.einsum("nhj,hij->nhi", values, d_state_b, preferred_element_type=jnp.float32) + d_norm
    d_val = jnp.einsum("nhi,hij->nhj", feat_k, d_state_b, preferred_element_type=jnp.float32)
    d_q = (d_fq * phi_slope(q_raw)).astype(jnp.bfloat16)
    d_k = (d_fk * phi_slope(k_raw)).astype(jnp.bfloat16)
    d_qkv = jnp.stack([d_q, d_k, d_val.astype(jnp.bfloat16)], axis=1).reshape(tokens, 3 * width)
    dwqkv_part = jnp.einsum("nc,nf->cf", normed, d_qkv, preferred_element_type=jnp.float32).reshape(width, 3, heads, head_dim)
    dw_qkv = lax.psum_scatter(dwqkv_part, "seq", scatter_dimension=0, tiled=True)
    d_normed = jnp.einsum("nf,cf->nc", d_qkv, w_flat, preferred_element_type=jnp.float32)
    d_gamma, d_beta = lax.psum((jnp.sum(d_normed * x_hat, axis=0), jnp.sum(d_normed, axis=0)), "seq")
    scaled_grad = d_normed * ln_gamma
    d_ln = inv_std * (scaled_grad - jnp.mean(scaled_grad, axis=-1, keepdims=True) - x_hat * jnp.mean(scaled_grad * x_hat, axis=-1, keepdims=True))
    dx_tok = (dy_tok.astype(jnp.float32) + d_ln).astype(jnp.bfloat16)
    return y_tok, dx_tok, dw_qkv, dw_out, d_gamma, d_beta


def solution(mesh):
    rows = P(("data", "seq"), None)
    return jax.shard_map(
        local_block, mesh=mesh,
        in_specs=(rows, rows, P(None), P(None), P(None, None, None, None), P(None, None)),
        out_specs=(rows, rows, P(("data", "seq"), None, None, None), rows, P("data"), P("data")),
        check_vma=False)
```

profile of v0, /device:TPU:22, one launch (start us, length us, event | category | flops | bytes accessed | tf_op | source)
XLA Modules:
  0.0 451.5 jit_solution(9053273174462688051)
XLA Ops:
  7.3 3.0 convert_reduce_fusion
  10.3 3.0 fusion.16
  13.3 19.1 %convolution_convert_fusion = bf16[2048,3072]{1,0:T(8,128)(2,1)} fusion(bf16[1024,3072]{0,1:T(8,128)(2,1)} %bitcast.124, bf16[2048,1024]{1,0:T(8,128)(2,1)S(1)} %copy-done.1, f32[1024]{0:T(1024)S(1)} %copy-done.6, f32[1024]{0:T(1024)S(1)} %copy-done.5, f32[2048]{0:T(1024)S(1)} %add_rsqrt_fusion, f32[2048]{0:T(1024)S(1)} %broadcast_multiply_fusion.2), kind=kOutput, calls=%fused_computation.12 | convolution fusion | flops 12903776256 | bytes 23093248 | tf_op jit(solution)/shard_map/dot_general | solution.py:27
  32.4 16.7 %copy.19 = bf16[2048,3072]{0,1:T(8,128)(2,1)} copy(bf16[2048,3072]{1,0:T(8,128)(2,1)} %convolution_convert_fusion) | data formatting | bytes 25165824 | tf_op jit(solution)/shard_map/convert_element_type | solution.py:27
  49.1 3.9 convert_reduce_fusion.1
  53.0 5.7 %fusion.37 = f32[16,64,64]{2,1,0:T(8,128)S(1)} fusion(bf16[2048,3,16,64]{0,3,2,1:T(8,128)(2,1)} %bitcast.112), kind=kOutput, calls=%fused_computation.58 | convolution fusion | flops 281018368 | bytes 8650752 | tf_op jit(solution)/shard_map/nhi,nhj->hij/dot_general | solution.py:34
  58.8 58.8 %all-reduce.5 = (bf16[16,64]{1,0:T(8,128)(2,1)S(1)}, bf16[16,64,64]{2,1,0:T(8,128)(2,1)S(1)}) all-reduce(f32[16,64]{1,0:T(8,128)S(1)} %convert_reduce_fusion.1, f32[16,64,64]{2,1,0:T(8,128)S(1)} %fusion.37), channel_id=1, replica_groups=mesh['data'=4,'seq'=16] {'seq'}, use_global_device_ids=true, to_apply=%region_4.5 | all-reduce | flops 66560 | bytes 399360 | tf_op jit(solution)/shard_map/psum | solution.py:36
  117.6 4.5 fusion.44
  122.1 4.5 %fusion.56 = f32[2048,1024]{0,1:T(8,128)S(1)} fusion(bf16[2048,1024]{1,0:T(8,128)(2,1)S(1)} %copy-done.4, bf16[1024,1024]{1,0:T(8,128)(2,1)S(1)} %copy-done), kind=kOutput, calls=%fused_computation.77 | convolution fusion | flops 4294967296 | bytes 14680064 | tf_op jit(solution)/shard_map/nd,cd->nc/dot_general | solution.py:46
  126.7 6.5 %multiply_reduce_fusion.1 = (f32[2048,16]{0,1:T(8,128)S(1)}, bf16[2048,16,64]{0,2,1:T(8,128)(2,1)}, bf16[2048,16,64]{0,2,1:T(8,128)(2,1)}) fusion(f32[2048,16,64]{0,2,1:T(8,128)S(1)} %bitcast.125, f32[2048,16]{0,1:T(8,128)S(1)} %bitcast.122, bf16[16,64,64]{2,1,0:T(8,128)(2,1)S(1)} %get-tuple-element.27, bf16[2048,3,16,64]{0,3,2,1:T(8,128)(2,1)S(1)} %bitcast.118), kind=kOutput, calls=%fused_computation.48 | convolution fusion | flops 295665664 | bytes 21495808 | tf_op jit(solution)/shard_map/nhi,hij->nhj/dot_general | solution.py:39
  135.8 4.2 fusion.52
  140.0 5.1 %fusion.38 = bf16[2048,1,16,64]{0,3,2,1:T(8,128)(2,1)} fusion(bf16[2048,3,16,64]{0,3,2,1:T(8,128)(2,1)S(1)} %bitcast.121, f32[16,64]{1,0:T(8,128)S(1)} %convert_element_type.225, f32[2048,16]{0,1:T(8,128)S(1)} %get-tuple-element.28, bf16[2048,16,64]{0,2,1:T(8,128)(2,1)S(1)} %copy-done.10, bf16[16,64,64]{2,1,0:T(8,128)(2,1)S(1)} %get-tuple-element.27), kind=kOutput, calls=%fused_computation.59 | convolution fusion | flops 285212672 | bytes 12849152 | tf_op jit(solution)/shard_map/nhj,hij->nhi/dot_general | solution.py:49
  145.1 52.0 %all-reduce.6 = (bf16[16,64,64]{2,1,0:T(8,128)(2,1)S(1)}, f32[16,64]{1,0:T(8,128)S(1)}) all-reduce(f32[16,64,64]{2,1,0:T(8,128)S(1)} %fusion.52, f32[16,64]{1,0:T(8,128)S(1)} %neg.3), channel_id=1, replica_groups=mesh['data'=4,'seq'=16] {'seq'}, use_global_device_ids=true, to_apply=%region_6.7 | all-reduce | flops 66560 | bytes 401408 | tf_op jit(solution)/shard_map/psum | solution.py:52
  197.2 5.2 %convert_bitcast_fusion = bf16[2048,1,16,64]{0,3,2,1:T(8,128)(2,1)S(1)} fusion(bf16[16,64,64]{2,1,0:T(8,128)(2,1)S(1)} %get-tuple-element.24, bf16[2048,3,16,64]{0,3,2,1:T(8,128)(2,1)} %bitcast.114), kind=kOutput, calls=%fused_computation.57 | convolution fusion | flops 283115520 | bytes 8519680 | tf_op jit(solution)/shard_map/nhi,hij->nhj/dot_general | solution.py:55
  202.4 7.5 %fusion.39 = bf16[2048,1,16,64]{0,3,2,1:T(8,128)(2,1)S(1)} fusion(bf16[2048,3,16,64]{0,3,2,1:T(8,128)(2,1)} %bitcast.115, f32[16,64]{1,0:T(8,128)S(1)} %get-tuple-element.25, bf16[16,64,64]{2,1,0:T(8,128)(2,1)S(1)} %get-tuple-element.24), kind=kOutput, calls=%fused_computation.60 | convolution fusion | flops 283115520 | bytes 12718080 | tf_op jit(solution)/shard_map/nhj,hij->nhi/dot_general | solution.py:54
  211.8 33.5 %fusion = f32[1024,3,16,64]{3,0,2,1:T(8,128)} fusion(bf16[2048,1,16,64]{0,3,2,1:T(8,128)(2,1)S(1)} %convert_bitcast_fusion, bf16[2048,1,16,64]{0,3,2,1:T(8,128)(2,1)S(1)} %fusion.39, bf16[2048,1,16,64]{0,3,2,1:T(8,128)(2,1)S(1)} %copy-done.9, bf16[2048,1024]{1,0:T(8,128)(2,1)S(1)} %copy-done.2, f32[1024]{0:T(1024)S(1)} %copy-done.6, f32[1024]{0:T(1024)S(1)} %copy-done.5, ...), kind=kOutput, calls=%fused_computation.1 | convolution fusion | flops 12935233536 | bytes 29384704 | tf_op jit(solution)/shard_map/nc,nf->cf/dot_general | solution.py:59
  245.7 9.9 %fusion.57 = f32[1024,1024]{1,0:T(8,128)} fusion(bf16[2048,1024]{0,1:T(8,128)(2,1)} %bitcast.126, bf16[2048,1024]{1,0:T(8,128)(2,1)} %param.7), kind=kOutput, calls=%fused_computation.78 | convolution fusion | flops 4294967296 | bytes 12582912 | tf_op jit(solution)/shard_map/nc,nd->cd/dot_general | solution.py:44
  255.6 21.8 %fusion.15 = (f32[1024]{0:T(1024)S(1)}, f32[2048]{0:T(1024)S(1)}, f32[2048]{0:T(1024)S(1)}, f32[1024]{0:T(1024)S(1)}, f32[2048,1024,1,1]{1,0,3,2:T(8,128)}) fusion(bf16[2048,1024]{1,0:T(8,128)(2,1)} %param.6, f32[2048]{0:T(1024)S(1)} %add_rsqrt_fusion, f32[2048]{0:T(1024)S(1)} %broadcast_multiply_fusion.2, f32[1024]{0:T(1024)S(1)} %copy-done.5, ...), kind=kOutput, calls=%fused_computation.26 | convolution fusion | flops 12918450176 | bytes 31502336 | tf_op jit(solution)/shard_map/nf,cf->nc/dot_general | solution.py:61
  277.4 25.4 %all-reduce = (f32[1024]{0:T(1024)}, f32[1024]{0:T(1024)}) all-reduce(f32[1024]{0:T(1024)S(1)} %get-tuple-element.18, f32[1024]{0:T(1024)S(1)} %get-tuple-element.21), channel_id=1, replica_groups=mesh['data'=4,'seq'=16] {'seq'}, use_global_device_ids=true, to_apply=%region_14.15 | all-reduce | flops 2048 | bytes 16384 | tf_op jit(solution)/shard_map/psum | solution.py:62
  302.8 10.7 %fusion.14 = bf16[2048,1024]{1,0:T(8,128)(2,1)} fusion(bf16[2048,1024]{1,0:T(8,128)(2,1)} %param.6, bf16[2048,1024]{1,0:T(8,128)(2,1)} %param.7, f32[2048,1024,1,1]{1,0,3,2:T(8,128)} %get-tuple-element.32, f32[2048]{0:T(1024)S(1)} %get-tuple-element.33, f32[2048]{0:T(1024)S(1)} %get-tuple-element.34, f32[1024]{0:T(1024)S(1)} %copy-done.5, ...), kind=kLoop, calls=%fused_computation.25 | loop fusion | flops 23068672 | bytes 21008384 | tf_op jit(solution)/shard_map/convert_element_type | solution.py:65
  313.5 6.4 %fusion.17 = bf16[2048,1024]{1,0:T(8,128)(2,1)} fusion(bf16[2048,1024]{1,0:T(8,128)(2,1)S(1)} %copy-done.3, bf16[2048,1024]{0,1:T(8,128)(2,1)S(1)} %bitcast.127, bf16[1024,1024]{1,0:T(8,128)(2,1)S(1)} %copy-done), kind=kOutput, calls=%fused_computation.28 | convolution fusion | flops 4301258752 | bytes 14680064 | tf_op jit(solution)/shard_map/dot_general | solution.py:43
  319.8 62.9 %reduce-scatter.3.cloned.1.call-done = f32[64,3,16,64]{3,0,2,1:T(8,128)} async-done(((f32[1024,3,16,64]{3,0,2,1:T(8,128)}), f32[64,3,16,64]{3,0,2,1:T(8,128)}) %reduce-scatter.3.cloned.1.call-update) | async-done | bytes 786448 | tf_op jit(solution)/shard_map/reduce_scatter | solution.py:60
  382.8 3.5 copy.23
  386.2 58.0 %reduce-scatter.5.cloned.1.call-done = f32[64,1024]{1,0:T(8,128)} async-done(((f32[1024,1024]{1,0:T(8,128)}), f32[64,1024]{1,0:T(8,128)}) %reduce-scatter.5.cloned.1.call-update) | async-done | bytes 262160 | tf_op jit(solution)/shard_map/reduce_scatter | solution.py:45
  (42 shorter events, 5.1 us)
Async XLA Ops:
  7.2 114.9 %copy-start = (bf16[1024,1024]{1,0:T(8,128)(2,1)S(1)}, bf16[1024,1024]{1,0:T(8,128)(2,1)}, u32[]{:S(2)}) copy-start(bf16[1024,1024]{1,0:T(8,128)(2,1)} %param.11) | copy-start | bytes 6291460
  7.2 6.1 %copy-start.5 = (f32[1024]{0:T(1024)S(1)}, f32[1024]{0:T(1024)}, u32[]{:S(2)}) copy-start(f32[1024]{0:T(1024)} %param.8) | copy-start | bytes 12292
  7.2 6.1 %copy-start.6 = (f32[1024]{0:T(1024)S(1)}, f32[1024]{0:T(1024)}, u32[]{:S(2)}) copy-start(f32[1024]{0:T(1024)} %param.9) | copy-start | bytes 12292
  7.2 375.6 %reduce-scatter.3.cloned.1.call-start = ((), (), s32[]{:S(2)}) async-start(), calls=%async_computation.2 | async-start | bytes 26738688 | tf_op jit(solution)/shard_map/reduce_scatter | solution.py:60
  7.3 6.1 %copy-start.1 = (bf16[2048,1024]{1,0:T(8,128)(2,1)S(1)}, bf16[2048,1024]{1,0:T(8,128)(2,1)}, u32[]{:S(2)}) copy-start(bf16[2048,1024]{1,0:T(8,128)(2,1)} %param.6) | copy-start | bytes 12582916
  117.5 4.6 %copy-start.4 = (bf16[2048,1024]{1,0:T(8,128)(2,1)S(1)}, bf16[2048,1024]{1,0:T(8,128)(2,1)}, u32[]{:S(2)}) copy-start(bf16[2048,1024]{1,0:T(8,128)(2,1)} %param.7) | copy-start | bytes 12582916
  117.6 9.1 %slice-start = ((s8[12582912]{0:T(1024)(128)(4,1)}), s8[4194304]{0:T(1024)(128)(4,1)S(1)}, s32[]{:S(2)}) async-start(s8[12582912]{0:T(1024)(128)(4,1)} %bitcast.116), calls=%async_computation.4 | async-start | bytes 8388608
  122.1 4.6 %slice-start.1 = ((s8[12582912]{0:T(1024)(128)(4,1)}), s8[4194304]{0:T(1024)(128)(4,1)S(1)}, s32[]{:S(2)}) async-start(s8[12582912]{0:T(1024)(128)(4,1)} %bitcast.116), calls=%async_computation.5 | async-start | bytes 8388608
  122.1 4.6 %slice-start.2 = ((s8[12582912]{0:T(1024)(128)(4,1)}), s8[4194304]{0:T(1024)(128)(4,1)S(1)}, s32[]{:S(2)}) async-start(s8[12582912]{0:T(1024)(128)(4,1)} %bitcast.116), calls=%async_computation.6 | async-start | bytes 8388608
  135.8 4.2 copy-start.10
  202.3 7.5 %copy-start.8 = (bf16[2048,1,16,64]{0,3,2,1:T(8,128)(2,1)}, bf16[2048,1,16,64]{0,3,2,1:T(8,128)(2,1)S(1)}, u32[]{:S(2)}) copy-start(bf16[2048,1,16,64]{0,3,2,1:T(8,128)(2,1)S(1)} %convert_bitcast_fusion) | copy-start | bytes 12582916
  202.3 9.5 %copy-start.2 = (bf16[2048,1024]{1,0:T(8,128)(2,1)S(1)}, bf16[2048,1024]{1,0:T(8,128)(2,1)}, u32[]{:S(2)}) copy-start(bf16[2048,1024]{1,0:T(8,128)(2,1)} %param.6) | copy-start | bytes 12582916
  202.4 9.4 %copy-start.9 = (bf16[2048,1,16,64]{0,3,2,1:T(8,128)(2,1)S(1)}, bf16[2048,1,16,64]{0,3,2,1:T(8,128)(2,1)}, u32[]{:S(2)}) copy-start(bf16[2048,1,16,64]{0,3,2,1:T(8,128)(2,1)} %fusion.38) | copy-start | bytes 12582916
  209.9 1.9 copy-start.11
  245.3 198.9 %reduce-scatter.5.cloned.1.call-start = ((), (), s32[]{:S(2)}) async-start(), calls=%async_computation.3 | async-start | bytes 4456448 | tf_op jit(solution)/shard_map/reduce_scatter | solution.py:45
  302.8 10.7 %copy-start.3 = (bf16[2048,1024]{1,0:T(8,128)(2,1)S(1)}, bf16[2048,1024]{1,0:T(8,128)(2,1)}, u32[]{:S(2)}) copy-start(bf16[2048,1024]{1,0:T(8,128)(2,1)} %param.6) | copy-start | bytes 12582916
  302.8 10.7 %copy-start.7 = (bf16[2048,16,64]{0,2,1:T(8,128)(2,1)S(1)}, bf16[2048,16,64]{0,2,1:T(8,128)(2,1)}, u32[]{:S(2)}) copy-start(bf16[2048,16,64]{0,2,1:T(8,128)(2,1)} %get-tuple-element.30) | copy-start | bytes 12582916
Sparse Core Ops, SparseCore 0:
  245.5 137.2 reduce-scatter.2
  385.7 58.5 reduce-scatter.4
where the time goes:
time: 458 us; the launch traced here: 452 us
  blocking collectives  136 us (30%)
  matrix products  134 us (29%)
  waiting for transfers between devices  121 us (26%)
  other arithmetic  23.2 us (5%)
  local copies, waits for them, and re-layouts  22.2 us (5%)
  between operations  14.8 us (3%)
    reduce_scatter x1, waiting for transfers between devices, local_block(): lax.psum_scatter(dwqkv_part, 'seq', scatter_dimension=0, tiled=True)  62.9 us
    psum x1, blocking collectives, local_block(): state, norm_vec = lax.psum((state_part, norm_part), 'seq')  58.8 us
    reduce_scatter x1, waiting for transfers between devices, local_block(): lax.psum_scatter(dwout_part, 'seq', scatter_dimension=0, tiled=True)  58 us
    psum x1, blocking collectives, local_block(): d_state, d_norm = lax.psum((dstate_part, dnorm_part), 'seq')  52 us
    dot_general x1, matrix products, local_block(): jnp.einsum('nc,nf->cf', normed, d_qkv, preferred_element_type=jnp.float32)  33.5 us
    psum x1, blocking collectives, local_block(): lax.psum((jnp.sum(d_normed * x_hat, axis=0), jnp.sum(d_normed, axis=0)),...  25.4 us
    dot_general x1, matrix products, local_block(): jnp.einsum('nf,cf->nc', d_qkv, w_flat, preferred_element_type=jnp.float32)  21.8 us
    dot_general x1, matrix products, local_block(): jnp.dot(normed, w_flat, preferred_element_type=jnp.float32)  19.1 us
  transfers between devices with their start and end apart: 2, of which 2 were waited for; matrix products, arithmetic and copies ran while one was open for 12% of the time, Pallas kernels for 0%

commit v1 on v0

v1 whole, which is shorter than its diff:
```python
import functools

import jax
import jax.numpy as jnp
from jax import lax
from jax.experimental import pallas as pl
from jax.experimental.pallas import tpu as pltpu
from jax.sharding import PartitionSpec as P

LN_EPS = 1e-5
MESH = pl.DeviceIdType.MESH
BF = jnp.bfloat16
F32 = jnp.float32
TILE = 256
GROUP = 256
PIECE = 40
VMEM_LIMIT = 66 * 1024 * 1024 - 2 * 1024 * 1024 - 65536

NN = (((1,), (0,)), ((), ()))
NT = (((1,), (1,)), ((), ()))
TN = (((0,), (0,)), ((), ()))


def dot(a, b, dims=NN):
    return lax.dot_general(a, b, dims, preferred_element_type=F32)


def phi_act(t):
    return jnp.where(t > 0, t + 1.0, jnp.exp(jnp.minimum(t, 0.0)))


def phi_slope(t):
    return jnp.where(t > 0, 1.0, jnp.exp(jnp.minimum(t, 0.0)))


def cols(i, size):
    return pl.ds(pl.multiple_of(i * size, size), size)


class Where:
    def __init__(self, n):
        me = lax.axis_index("seq")
        self.chips = n // 2
        self.chip = me // 2
        self.core = lax.rem(me, 2)

    def at(self, offset):
        return {"seq": lax.rem(self.chip + offset + self.chips, self.chips) * 2 + self.core}

    def partner(self):
        return {"seq": self.chip * 2 + 1 - self.core}

    def source(self, offset):
        return lax.rem(self.chip + offset + self.chips, self.chips)

    def barrier(self):
        sem = pltpu.get_barrier_semaphore()
        for k in range(1, self.chips):
            pl.semaphore_signal(sem, inc=1, device_id=self.at(k), device_id_type=MESH)
        pl.semaphore_signal(sem, inc=1, device_id=self.partner(), device_id_type=MESH)
        pl.semaphore_wait(sem, self.chips)


def remote(src, dst, send, recv, device):
    return pltpu.make_async_remote_copy(
        src_ref=src, dst_ref=dst, send_sem=send, recv_sem=recv, device_id=device, device_id_type=MESH)


class StateSum:
    def __init__(self, w, part, pair, recv, fin, ssem, rsem):
        self.w, self.part, self.pair, self.recv, self.fin = w, part, pair, recv, fin
        self.ssem, self.rsem = ssem, rsem
        m = w.chips
        self.c0 = remote(part.at[1 - w.core], pair, ssem.at[0], rsem.at[0], w.partner())
        self.c1 = [remote(pair.at[w.source(k)], recv.at[k], ssem.at[k], rsem.at[k], w.at(k)) for k in range(1, m)]
        self.c2 = [
            remote(fin.at[w.core, w.chip], fin.at[w.core, w.chip], ssem.at[m + k], rsem.at[m + k], w.at(k))
            for k in range(1, m)]
        self.c3 = remote(fin.at[w.core], fin.at[w.core], ssem.at[m], rsem.at[m], w.partner())

    def start(self):
        self.c0.start()

    def exchange(self):
        w = self.w
        self.c0.wait()
        self.pair[...] = self.pair[...] + self.part[w.core]
        for c in self.c1:
            c.start()

    def own(self):
        w = self.w
        total = self.pair[w.chip]
        for k, c in enumerate(self.c1, 1):
            c.wait_recv()
            total = total + self.recv[k]
        self.fin[w.core, w.chip] = total
        for c in self.c2:
            c.start()

    def finish(self):
        for c in self.c2:
            c.wait_recv()
        self.c3.start()
        for c in self.c1 + self.c2:
            c.wait_send()
        self.c3.wait()


def put_state(part, g, state, vec):
    lane = lax.broadcasted_iota(jnp.int32, (64, 128), 1)
    for mm in range(2):
        block = state[128 * mm:128 * mm + 128, 128 * mm:128 * mm + 128]
        both = jnp.where(lane < 64, block[0:64], block[64:128])
        row = vec[:, 128 * mm:128 * mm + 128]
        for half in range(2):
            part[half, 2 * g + mm, 0:32, :] = both[32 * half:32 * half + 32]
            part[half, 2 * g + mm, 32:40, :] = row


def get_state(fin, m):
    both = jnp.concatenate([fin[0, m, 0:32, :], fin[1, m, 0:32, :]], axis=0)
    lane = lax.broadcasted_iota(jnp.int32, (64, 128), 1)
    block = jnp.concatenate([jnp.where(lane < 64, both, 0.0), jnp.where(lane < 64, 0.0, both)], axis=0)
    return block, fin[0, m, 32:40, :]


def spread(row):
    return jnp.transpose(jnp.concatenate([row] * 16, axis=0))


def norm_rows(x):
    x = x.astype(F32)
    centered = x - jnp.mean(x, axis=-1, keepdims=True)
    inv_std = lax.rsqrt(jnp.mean(centered * centered, axis=-1, keepdims=True) + LN_EPS)
    return centered * inv_std, inv_std


def front(n, x_hbm, dy_hbm, gamma_ref, beta_ref, wt_hbm, wo_hbm,
          ut_hbm, q_hbm, k_hbm, v_hbm, do_hbm, fin_out,
          x, dy, wt, wo, u, ut, q, k, v, do, part, pair, recv, fin, ssem, rsem, lsem, xsem, osem):
    w = Where(n)
    tokens, width = x.shape
    tiles, groups = tokens // TILE, width // GROUP
    state = StateSum(w, part, pair, recv, fin, ssem, rsem)

    def x_copy(t):
        return pltpu.make_async_copy(x_hbm.at[pl.ds(t * TILE, TILE)], x.at[pl.ds(t * TILE, TILE)], xsem.at[t])

    loads = [
        pltpu.make_async_copy(wt_hbm.at[pl.ds(width, 2 * width)], wt.at[pl.ds(width, 2 * width)], lsem.at[0]),
        pltpu.make_async_copy(wt_hbm.at[pl.ds(0, width)], wt.at[pl.ds(0, width)], lsem.at[1]),
        pltpu.make_async_copy(wo_hbm, wo, lsem.at[2]),
        pltpu.make_async_copy(dy_hbm, dy, lsem.at[3]),
    ]
    x_copy(0).start()
    loads[0].start()
    for t in range(1, tiles):
        x_copy(t).start()
    for c in loads[1:]:
        c.start()
    w.barrier()
    loads[0].wait()

    def kv_tile(t, carry):
        x_copy(t).wait()

        def rows(r, c):
            at = pl.ds(pl.multiple_of(r * 64, 64), 64)
            x_hat, _ = norm_rows(x[pl.ds(pl.multiple_of(t * TILE + r * 64, 64), 64), :])
            u[at, :] = (x_hat * gamma_ref[...] + beta_ref[...]).astype(BF)
            return c

        lax.fori_loop(0, TILE // 64, rows, 0)
        ut[:, cols(t, TILE)] = jnp.transpose(u[...])
        k[:, cols(t, TILE)] = dot(wt[width:2 * width], u[...], NT).astype(BF)
        v[:, cols(t, TILE)] = dot(wt[2 * width:3 * width], u[...], NT).astype(BF)
        return carry

    lax.fori_loop(0, tiles, kv_tile, 0)
    outs = [
        pltpu.make_async_copy(ut, ut_hbm, osem.at[0]),
        pltpu.make_async_copy(k, k_hbm, osem.at[1]),
        pltpu.make_async_copy(v, v_hbm, osem.at[2]),
        pltpu.make_async_copy(q, q_hbm, osem.at[3]),
        pltpu.make_async_copy(do, do_hbm, osem.at[4]),
    ]
    for c in outs[:3]:
        c.start()

    ones = jnp.ones((16, tokens), BF)
    for g in range(groups):
        at = slice(g * GROUP, (g + 1) * GROUP)
        fk = phi_act(k[at, :].astype(F32)).astype(BF)
        put_state(part, g, dot(fk, v[at, :], NT), dot(ones, fk, NT)[0:8])
    state.start()
    loads[1].wait()

    def q_tile(t, carry):
        q[:, cols(t, TILE)] = dot(wt[0:width], ut[:, cols(t, TILE)]).astype(BF)
        return carry

    def do_tile(t, carry):
        do[:, cols(t, TILE)] = dot(wo[...], dy[pl.ds(pl.multiple_of(t * TILE, TILE), TILE), :], NT)
        return carry

    early = tiles // 4
    lax.fori_loop(0, early, q_tile, 0)
    state.exchange()
    lax.fori_loop(early, tiles, q_tile, 0)
    outs[3].start()
    loads[2].wait()
    loads[3].wait()
    lax.fori_loop(0, early, do_tile, 0)
    state.own()
    lax.fori_loop(early, tiles, do_tile, 0)
    outs[4].start()
    state.finish()
    fin_out[...] = fin[...]
    for c in outs:
        c.wait()


class Ring:
    def __init__(self, w, blk, pair, recv, dssem, drsem, ssem, rsem, outs):
        self.w, self.blk, self.pair, self.recv = w, blk, pair, recv
        self.ssem, self.rsem, self.outs = ssem, rsem, outs
        self.d2d = [
            remote(blk.at[b % 2, :, 1 - w.core], pair.at[b], dssem.at[b], drsem.at[b], w.partner())
            for b in range(len(outs))]
        self.queue, self.pending, self.sent, self.freed = [], [], [], set()

    def copy(self, b, s, d):
        w, steps = self.w, self.w.chips - 1
        lanes = pl.ds(256 * d, 256)
        sem = (b * steps + s) * 2 + d
        to = w.at(1) if d == 0 else w.at(-1)
        if s == 0:
            src = self.pair.at[b, w.source(-1 if d == 0 else 1), :, lanes]
        else:
            src = self.recv.at[b, s - 1, d]
        return remote(src, self.recv.at[b, s, d], self.ssem.at[sem], self.rsem.at[sem], to)

    def free(self, b):
        if b >= 0 and b not in self.freed:
            while b in self.pending:
                self.join()
            self.d2d[b].wait_send()
            self.freed.add(b)

    def block(self, b):
        self.d2d[b].start()
        self.pending.append(b)

    def join(self):
        b = self.pending.pop(0)
        w = self.w
        self.d2d[b].wait_recv()
        for j in range(w.chips):
            self.pair[b, j] = self.pair[b, j] + self.blk[b % 2, j, w.core]
        for d in range(2):
            c = self.copy(b, 0, d)
            c.start()
            self.sent.append(c)
        self.queue.append((b, 0))

    def step(self):
        b, s = self.queue.pop(0)
        w, last = self.w, self.w.chips - 2
        for d in range(2):
            lanes = slice(256 * d, 256 * d + 256)
            self.copy(b, s, d).wait_recv()
            j = w.source(-2 - s if d == 0 else 2 + s) if s < last else w.chip
            total = self.recv[b, s, d] + self.pair[b, j, :, lanes]
            if s == last:
                out, first = self.outs[b]
                out[:, first + 256 * d:first + 256 * d + 256] = total
            else:
                self.recv[b, s, d] = total
                c = self.copy(b, s + 1, d)
                c.start()
                self.sent.append(c)
        if s < last:
            self.queue.append((b, s + 1))

    def tick(self, steps=2, fresh=0):
        while len(self.pending) > fresh:
            self.join()
        for _ in range(min(steps, len(self.queue))):
            self.step()

    def drain(self, blocks):
        while self.pending:
            self.join()
        while self.queue:
            self.step()
        for b in range(blocks):
            self.free(b)
        for c in self.sent:
            c.wait_send()


def back(n, x_hbm, dy_hbm, gamma_ref, beta_ref, wt_hbm, wo_hbm, ut_hbm, q_hbm, k_hbm, v_hbm, do_hbm, sfin,
         y_hbm, dx_hbm, dwq_out, dwo_out, dg_out, db_out,
         big, wo, ut, q, k, v, do, xt, dyt, ot, du, sbd, sbdt, zrow, zcol, rden, dzacc, gacc, bacc,
         part, pair, recv, fin, blk, rpair, rrecv, gb, gpair, gall,
         ssem, rsem, dssem, drsem, rssem, rrsem, gssem, grsem, lsem, qsem, dosem, xsem, dysem, osem):
    w = Where(n)
    width, tokens = q.shape
    half = tokens // 2
    tiles, groups = tokens // TILE, width // GROUP
    chunk = do.shape[2]
    chunks = tokens // chunk
    streams = width // 512

    def q_copy(i):
        return pltpu.make_async_copy(q_hbm.at[:, pl.ds(i * chunk, chunk)], q.at[:, pl.ds(i * chunk, chunk)], qsem.at[i])

    def do_copy(i):
        return pltpu.make_async_copy(do_hbm.at[:, pl.ds(i * chunk, chunk)], do.at[i % 2], dosem.at[i % 2])

    dy_loads = [pltpu.make_async_copy(dy_hbm.at[pl.ds(i * half, half)], big.at[2 + i], lsem.at[i]) for i in range(2)]
    ut_load = pltpu.make_async_copy(ut_hbm, ut, lsem.at[2])
    k_load = pltpu.make_async_copy(k_hbm, k, lsem.at[3])
    v_load = pltpu.make_async_copy(v_hbm, v, lsem.at[4])
    wo_load = pltpu.make_async_copy(wo_hbm, wo, lsem.at[5])
    wt_loads = [pltpu.make_async_copy(wt_hbm.at[pl.ds(i * width, width)], big.at[i], lsem.at[6 + i]) for i in range(3)]
    for i in range(chunks):
        q_copy(i).start()
    for c in dy_loads:
        c.start()
    do_copy(0).start()
    do_copy(1).start()
    for c in (ut_load, wo_load, k_load, v_load):
        c.start()
    w.barrier()

    outs = ([(dwo_out, 512 * i) for i in range(streams)]
            + [(dwq_out, 512 * i) for i in range(3 * streams)])
    ring = Ring(w, blk, rpair, rrecv, dssem, drsem, rssem, rrsem, outs)
    state = StateSum(w, part, pair, recv, fin, ssem, rsem)

    sbd[...] = jnp.zeros_like(sbd)
    sbdt[...] = jnp.zeros_like(sbdt)

    def build(source, with_rows):
        for m in range(w.chips):
            g, at = m // 2, slice(128 * (m % 2), 128 * (m % 2) + 128)
            block, row = get_state(source, m)
            sbd[g, at, at] = block.astype(BF)
            sbdt[g, at, at] = jnp.transpose(block).astype(BF)
            if with_rows:
                row = row.astype(BF).astype(F32)
                head = lax.broadcasted_iota(jnp.int32, (16, 128), 0) - 2 * (m % 2)
                lane = lax.broadcasted_iota(jnp.int32, (16, 128), 1) // 64
                zrow[g, :, at] = jnp.where(head == lane, jnp.concatenate([row, row], axis=0), 0.0).astype(BF)
            zcol[pl.ds(128 * m, 128), :] = spread(row)

    build(sfin, True)

    def attend(g, at):
        rows = cols(g, GROUP)
        qf = q[rows, at].astype(F32)
        fq = phi_act(qf).astype(BF)
        num = dot(sbdt[g], fq)
        return qf, fq, num

    for i in range(chunks):
        q_copy(i).wait()

        def o_group(g, carry, i=i):
            at = pl.ds(i * chunk, chunk)
            _, fq, num = attend(g, at)
            inv = 1.0 / dot(zrow[g], fq)[0:8]
            rden[g, :, at] = inv
            for r in range(4):
                a = num[64 * r:64 * r + 64] * inv[r:r + 1]
                first = i * chunk % half
                big[i * chunk // half, pl.ds(pl.multiple_of(g * GROUP + 64 * r, 64), 64), first:first + chunk] = a.astype(BF)
            return carry

        lax.fori_loop(0, groups, o_group, 0)

    for c in dy_loads:
        c.wait()

    def store_block(b, p, value):
        blk[b % 2, :, :, :, cols(p, 256)] = value.reshape(w.chips, 2, width // (2 * w.chips), 256)

    for i in range(streams):
        b = i
        ring.free(b - 2)

        def wo_part(p, carry, i=i, b=b):
            at = cols(2 * i + p, 256)
            store_block(b, p, dot(big[0], big[2, :, at]) + dot(big[1], big[3, :, at]))
            return carry

        lax.fori_loop(0, 2, wo_part, 0)
        ring.block(b)
        ring.tick(0, 1)

    dzacc[...] = jnp.zeros_like(dzacc)
    for i in range(chunks):
        do_copy(i).wait()

        def dq_group(g, carry, i=i):
            at = pl.ds(i * chunk, chunk)
            rows = cols(g, GROUP)
            qf, fq, num = attend(g, at)
            gs, cs = [], []
            for r in range(4):
                inv = rden[g, r:r + 1, at]
                a = num[64 * r:64 * r + 64] * inv
                gr = (do[i % 2, pl.ds(pl.multiple_of(g * GROUP + 64 * r, 64), 64), :] * inv).astype(BF)
                gs.append(gr)
                cs.append(jnp.sum(gr.astype(F32) * a, axis=0, keepdims=True))
            gg = jnp.concatenate(gs, axis=0)
            dfq = dot(sbd[g], gg)
            ds = dot(fq, gg, NT)
            at_g = cols(g, GROUP)
            du[:, at_g] = ds if i == 0 else du[:, at_g] + ds
            fqf = fq.astype(F32)
            for r in range(4):
                rr = slice(64 * r, 64 * r + 64)
                row = pl.ds(pl.multiple_of(g * GROUP + 64 * r, 64), 64)
                zc = zcol[row, :]
                total = dzacc[row, :]
                for j in range(chunk // 128):
                    lanes = slice(128 * j, 128 * j + 128)
                    c = cs[r][:, lanes]
                    qr = qf[rr, lanes]
                    dq = ((dfq[rr, lanes] - c * zc) * phi_slope(qr)).astype(BF)
                    q[row, pl.ds(i * chunk + 128 * j, 128)] = dq
                    total = total - c * fqf[rr, lanes]
                dzacc[row, :] = total
            return carry

        lax.fori_loop(0, groups, dq_group, 0)
        if i + 2 < chunks:
            do_copy(i + 2).start()
        ring.tick()

    for g in range(groups):
        rows = [jnp.sum(jnp.transpose(dzacc[pl.ds(g * GROUP + 128 * mm, 128), :]), axis=0, keepdims=True) for mm in range(2)]
        put_state(part, g, du[:, g * GROUP:(g + 1) * GROUP], jnp.broadcast_to(jnp.concatenate(rows, axis=1), (8, GROUP)))
    state.start()

    ut_load.wait()

    def grad_streams(first, d):
        for i in range(streams):
            b = first + i
            ring.free(b - 2)

            def part_of(p, carry, i=i, b=b):
                store_block(b, p, dot(ut[...], d[cols(2 * i + p, 256), :], NT))
                return carry

            lax.fori_loop(0, 2, part_of, 0)
            ring.block(b)
            if i == 0 and first == streams:
                state.exchange()
            ring.tick(fresh=1)

    grad_streams(streams, q)

    wo_load.wait()

    def x_copy(t, slot):
        return pltpu.make_async_copy(x_hbm.at[pl.ds(pl.multiple_of(t * TILE, TILE), TILE)], xt.at[slot], xsem.at[slot])

    def dy_copy(t, slot):
        return pltpu.make_async_copy(dy_hbm.at[pl.ds(pl.multiple_of(t * TILE, TILE), TILE)], dyt.at[slot], dysem.at[slot])

    def out_copy(hbm, t, slot):
        return pltpu.make_async_copy(ot.at[slot], hbm.at[pl.ds(pl.multiple_of(t * TILE, TILE), TILE)], osem.at[slot])

    x_copy(0, 0).start()
    for s in range(tiles // 2):
        def y_tile(t, carry):
            slot = lax.rem(t, 2)
            x_copy(t, slot).wait()

            @pl.when(t + 1 < tiles)
            def _():
                x_copy(t + 1, 1 - slot).start()

            @pl.when(t >= 2)
            def _():
                out_copy(y_hbm, t - 2, slot).wait()

            per = half // TILE
            at = cols(lax.rem(t, per), TILE)
            o = dot(big[lax.div(t, per), :, at], wo[...], TN)
            ot[slot] = (xt[slot].astype(F32) + o).astype(BF)
            out_copy(y_hbm, t, slot).start()
            return carry

        lax.fori_loop(2 * s, 2 * s + 2, y_tile, 0)
        if s == 0:
            state.own()
        ring.tick()
    out_copy(y_hbm, tiles - 2, 0).wait()
    out_copy(y_hbm, tiles - 1, 1).wait()
    for c in wt_loads:
        c.start()
    x_copy(0, 0).start()
    dy_copy(0, 0).start()
    state.finish()

    build(fin, False)
    k_load.wait()
    v_load.wait()
    for i in range(chunks):
        def dkv_group(g, carry, i=i):
            at = pl.ds(i * chunk, chunk)
            rows = cols(g, GROUP)
            kf = k[rows, at].astype(F32)
            fk = phi_act(kf).astype(BF)
            dv = dot(sbdt[g], fk).astype(BF)
            dfk = dot(sbd[g], v[rows, at])
            zc = zcol[rows, :]
            for j in range(chunk // 128):
                lanes = slice(128 * j, 128 * j + 128)
                k[rows, pl.ds(i * chunk + 128 * j, 128)] = ((dfk[:, lanes] + zc) * phi_slope(kf[:, lanes])).astype(BF)
            v[rows, at] = dv
            return carry

        lax.fori_loop(0, groups, dkv_group, 0)
        ring.tick()

    grad_streams(2 * streams, k)
    grad_streams(3 * streams, v)

    for c in wt_loads:
        c.wait()
    gacc[...] = jnp.zeros_like(gacc)
    bacc[...] = jnp.zeros_like(bacc)
    for s in range(tiles // 2):
        def dx_tile(t, carry):
            slot = lax.rem(t, 2)
            x_copy(t, slot).wait()
            dy_copy(t, slot).wait()

            @pl.when(t + 1 < tiles)
            def _():
                x_copy(t + 1, 1 - slot).start()
                dy_copy(t + 1, 1 - slot).start()

            @pl.when(t >= 2)
            def _():
                out_copy(dx_hbm, t - 2, slot).wait()

            at = cols(t, TILE)
            total = dot(q[:, at], big[0], TN) + dot(k[:, at], big[1], TN) + dot(v[:, at], big[2], TN)
            du[...] = total

            def rows(r, c):
                at = pl.ds(pl.multiple_of(r * 32, 32), 32)
                x_hat, inv_std = norm_rows(xt[slot, at, :])
                d = du[at, :]
                prod = d * x_hat
                gacc[...] += prod[0:8] + prod[8:16] + prod[16:24] + prod[24:32]
                bacc[...] += d[0:8] + d[8:16] + d[16:24] + d[24:32]
                e = d * gamma_ref[...]
                d_ln = inv_std * (e - jnp.mean(e, axis=-1, keepdims=True)
                                  - x_hat * jnp.mean(e * x_hat, axis=-1, keepdims=True))
                ot[slot, at, :] = (dyt[slot, at, :].astype(F32) + d_ln).astype(BF)
                return c

            lax.fori_loop(0, TILE // 32, rows, 0)
            out_copy(dx_hbm, t, slot).start()
            return carry

        lax.fori_loop(2 * s, 2 * s + 2, dx_tile, 0)
        ring.tick()

    gb[0] = gacc[...]
    gb[1] = bacc[...]
    swap = remote(gb, gpair, gssem.at[0], grsem.at[0], w.partner())
    swap.start()
    out_copy(dx_hbm, tiles - 2, 0).wait()
    out_copy(dx_hbm, tiles - 1, 1).wait()
    ring.tick()
    swap.wait()
    both = jnp.sum(gb[...] + gpair[...], axis=1, keepdims=True)
    gall[0] = jnp.broadcast_to(both, (2, 8, width))
    sends = [remote(gall.at[0], gall.at[j], gssem.at[j], grsem.at[j], w.at(j)) for j in range(1, w.chips)]
    for c in sends:
        c.start()
    ring.tick()
    ring.tick()
    for c in sends:
        c.wait()
    ring.drain(len(outs))
    total = gall[w.source(0)]
    for j in range(1, w.chips):
        total = total + gall[w.source(j)]
    dg_out[...] = total[0, 0:1]
    db_out[...] = total[1, 0:1]


def local_block(n, x_tok, dy_tok, ln_gamma, ln_beta, w_qkv, w_out):
    tokens, width = x_tok.shape
    chips = n // 2
    rows = width // n
    groups, tiles = width // GROUP, tokens // TILE
    chunk = min(512, tokens // 2)
    blocks = 4 * width // 512
    assert width // 128 == chips and w_qkv.shape[3] == 64
    wt = jnp.transpose(w_qkv, (1, 2, 3, 0)).reshape(3 * width, width)
    gamma, beta = ln_gamma.reshape(1, width), ln_beta.reshape(1, width)
    vmem, hbm = pl.BlockSpec(memory_space=pltpu.VMEM), pl.BlockSpec(memory_space=pl.ANY)
    dma = pltpu.SemaphoreType.DMA
    sums = [
        pltpu.VMEM((2, chips, PIECE, 128), F32),
        pltpu.VMEM((chips, PIECE, 128), F32),
        pltpu.VMEM((chips, PIECE, 128), F32),
        pltpu.VMEM((2, chips, PIECE, 128), F32),
    ]
    ut, q, k, v, do, fin = pl.pallas_call(
        functools.partial(front, n),
        name="front",
        out_shape=[jax.ShapeDtypeStruct((width, tokens), BF)] * 4
        + [jax.ShapeDtypeStruct((width, tokens), F32), jax.ShapeDtypeStruct((2, chips, PIECE, 128), F32)],
        in_specs=[hbm, hbm, vmem, vmem, hbm, hbm],
        out_specs=[hbm] * 5 + [vmem],
        scratch_shapes=[
            pltpu.VMEM((tokens, width), BF),
            pltpu.VMEM((tokens, width), BF),
            pltpu.VMEM((3 * width, width), BF),
            pltpu.VMEM((width, width), BF),
            pltpu.VMEM((TILE, width), BF),
            pltpu.VMEM((width, tokens), BF),
            pltpu.VMEM((width, tokens), BF),
            pltpu.VMEM((width, tokens), BF),
            pltpu.VMEM((width, tokens), BF),
            pltpu.VMEM((width, tokens), F32),
            *sums,
            dma((2 * chips,)), dma((2 * chips,)), dma((4,)), dma((tiles,)), dma((5,)),
        ],
        compiler_params=pltpu.CompilerParams(collective_id=0, has_side_effects=True, vmem_limit_bytes=VMEM_LIMIT),
    )(x_tok, dy_tok, gamma, beta, wt, w_out)
    steps = (chips - 1) * 2 * blocks
    y, dx, dwq, dwo, dg, db = pl.pallas_call(
        functools.partial(back, n),
        name="back",
        out_shape=[
            jax.ShapeDtypeStruct((tokens, width), BF),
            jax.ShapeDtypeStruct((tokens, width), BF),
            jax.ShapeDtypeStruct((rows, 3 * width), F32),
            jax.ShapeDtypeStruct((rows, width), F32),
            jax.ShapeDtypeStruct((1, width), F32),
            jax.ShapeDtypeStruct((1, width), F32),
        ],
        in_specs=[hbm, hbm, vmem, vmem, hbm, hbm, hbm, hbm, hbm, hbm, hbm, vmem],
        out_specs=[hbm, hbm, vmem, vmem, vmem, vmem],
        scratch_shapes=[
            pltpu.VMEM((4, width, tokens // 2), BF),
            pltpu.VMEM((width, width), BF),
            pltpu.VMEM((width, tokens), BF),
            pltpu.VMEM((width, tokens), BF),
            pltpu.VMEM((width, tokens), BF),
            pltpu.VMEM((width, tokens), BF),
            pltpu.VMEM((2, width, chunk), F32),
            pltpu.VMEM((2, TILE, width), BF),
            pltpu.VMEM((2, TILE, width), BF),
            pltpu.VMEM((2, TILE, width), BF),
            pltpu.VMEM((TILE, width), F32),
            pltpu.VMEM((groups, GROUP, GROUP), BF),
            pltpu.VMEM((groups, GROUP, GROUP), BF),
            pltpu.VMEM((groups, 16, GROUP), BF),
            pltpu.VMEM((width, 128), F32),
            pltpu.VMEM((groups, 8, tokens), F32),
            pltpu.VMEM((width, 128), F32),
            pltpu.VMEM((8, width), F32),
            pltpu.VMEM((8, width), F32),
            *sums,
            pltpu.VMEM((2, chips, 2, rows, 512), F32),
            pltpu.VMEM((blocks, chips, rows, 512), F32),
            pltpu.VMEM((blocks, chips - 1, 2, rows, 256), F32),
            pltpu.VMEM((2, 8, width), F32),
            pltpu.VMEM((2, 8, width), F32),
            pltpu.VMEM((chips, 2, 8, width), F32),
            dma((2 * chips,)), dma((2 * chips,)), dma((blocks,)), dma((blocks,)), dma((steps,)), dma((steps,)),
            dma((chips,)), dma((chips,)), dma((9,)), dma((tokens // chunk,)), dma((2,)), dma((2,)), dma((2,)), dma((2,)),
        ],
        compiler_params=pltpu.CompilerParams(collective_id=1, has_side_effects=True, vmem_limit_bytes=VMEM_LIMIT),
    )(x_tok, dy_tok, gamma, beta, wt, w_out, ut, q, k, v, do, fin)
    return (y, dx, dwq.reshape(rows, 3, w_qkv.shape[2], w_qkv.shape[3]), dwo, dg.reshape(width), db.reshape(width))


def solution(mesh):
    rows = P(("data", "seq"), None)
    return jax.shard_map(
        functools.partial(local_block, mesh.shape["seq"]), mesh=mesh,
        in_specs=(rows, rows, P(None), P(None), P(None, None, None, None), P(None, None)),
        out_specs=(rows, rows, P(("data", "seq"), None, None, None), rows, P("data"), P("data")),
        check_vma=False)
```

time: 458 us -> 229 us (0.50); the launches traced: 452 us -> 229 us
  Pallas kernels: 0 us -> 216 us
  blocking collectives: 136 us -> 0 us
  matrix products: 134 us -> 0 us
  waiting for transfers between devices: 121 us -> 0 us
  other arithmetic: 23.2 us -> 0 us
  between operations: 14.8 us -> 0.66 us
  local copies, waits for them, and re-layouts: 22.2 us -> 11.4 us
    pallas_call x0 -> x2, Pallas kernels: none -> 216 us  [the longest x1 171 us: local_block(): pl.pallas_call(functools.partial(back, n), name='back', out_shape=[jax.Sh...]
    psum x3 -> x0, blocking collectives: 136 us -> none  [the longest x1 58.8 us: local_block(): state, norm_vec = lax.psum((state_part, norm_part), 'seq')]
    dot_general x13 -> x0, matrix products: 134 us -> none  [the longest x1 33.5 us: local_block(): jnp.einsum('nc,nf->cf', normed, d_qkv, preferred_element_type=jnp.float32)]
    reduce_scatter x2 -> x0, waiting for transfers between devices: 121 us -> none  [the longest x1 62.9 us: local_block(): lax.psum_scatter(dwqkv_part, 'seq', scatter_dimension=0, tiled=True)]
    convert_element_type x1 -> x0, local copies, waits for them, and re-layouts: 16.7 us -> none  [local_block(): jnp.dot(normed, w_flat, preferred_element_type=jnp.float32)]
    reduce_sum x4 -> x0, other arithmetic: 12.5 us -> none  [the longest x1 3.9 us: local_block(): norm_part = jnp.sum(feat_k, axis=0, dtype=jnp.float32)]
    convert_element_type x2 -> x0, other arithmetic: 10.7 us -> none  [the longest x1 10.7 us: local_block(): dx_tok = (dy_tok.astype(jnp.float32) + d_ln).astype(jnp.bfloat16)]
  transfers between devices with their start and end apart: 2 -> 0, of which waited for: 2 -> 0; matrix products, arithmetic and copies ran while one was open for 12% -> 0% of each run, Pallas kernels for 0% -> 0%
where the time goes in v1:
time: 229 us
  Pallas kernels  216 us (94%)
  local copies, waits for them, and re-layouts  11.4 us (5%)
    pallas_call x1, Pallas kernels, local_block(): pl.pallas_call(functools.partial(back, n), name='back', out_shape=[jax.Sh...  171 us
    pallas_call x1, Pallas kernels, local_block(): pl.pallas_call(functools.partial(front, n), name='front', out_shape=[jax....  45.5 us
    unnamed x13, local copies, waits for them, and re-layouts  8.74 us

profile of v1, /device:TPU:22, one launch (start us, length us, event | category | flops | bytes accessed | tf_op | source)
XLA Modules:
  0.0 228.5 jit_solution(12572666235256413545)
XLA Ops:
  0.6 45.5 %front.1 = (bf16[1024,2048]{1,0:T(8,128)(2,1)}, bf16[1024,2048]{1,0:T(8,128)(2,1)}, bf16[1024,2048]{1,0:T(8,128)(2,1)}, bf16[1024,2048]{1,0:T(8,128)(2,1)}, f32[...) custom-call(bf16[2048,1024]{1,0:T(8,128)(2,1)} %x_hbm.3, bf16[2048,1024]{1,0:T(8,128)(2,1)} %dy_hbm.3, f32[1,1024]{1,0:T(1,128)} %bitcast.9, ...), custom_call_target="tpu_custom_call" | custom-call | tf_op jit(solution)/shard_map/front/pallas_call | solution.py:622
  46.2 170.9 %back.1 = (bf16[2048,1024]{1,0:T(8,128)(2,1)}, bf16[2048,1024]{1,0:T(8,128)(2,1)}, f32[64,3072]{1,0:T(8,128)}, f32[64,1024]{1,0:T(8,128)}, f32[1,1024]{1,0:T(1,128)}, /*index=5*/f32[1,1024]{1,0:T(1,128)}) custom-call(bf16[2048,1024]{1,0:T(8,128)(2,1)} %x_hbm.3, bf16[2048,1024]{1,0:T(8,128)(2,1)} %dy_hbm.3, f32[1,1024]{1,0:T(1,128)} %bitcast.10, ...), custom_call_target="tpu_custom_call" | custom-call | tf_op jit(solution)/shard_map/back/pallas_call | solution.py:646
  217.1 2.7 %reshape.33 = f32[64,3,16,64]{3,2,1,0:T(8,128)} reshape(f32[64,3072]{1,0:T(8,128)} %get-tuple-element.26) | data formatting | bytes 1572864 | tf_op jit(solution)/shard_map/reshape | solution.py:691
  219.8 0.0 copy-start
  219.8 4.8 %copy.17 = bf16[2048,1024]{1,0:T(8,128)(2,1)} copy(bf16[2048,1024]{1,0:T(8,128)(2,1)} %get-tuple-element.36) | data formatting | bytes 8388608
  224.6 0.0 copy-done
  224.6 0.0 copy-start.1
  224.6 0.0 copy-start.3
  224.6 0.0 copy-start.2
  224.6 2.0 copy.18
  226.6 0.0 copy-done.1
  226.6 0.7 copy.19
  227.3 0.0 copy-done.3
  227.3 0.6 copy.20
  227.9 0.0 copy-done.2
  227.9 0.6 copy.21
Async XLA Ops:
  219.8 4.8 %copy-start = (bf16[2048,1024]{1,0:T(8,128)(2,1)S(1)}, bf16[2048,1024]{1,0:T(8,128)(2,1)}, u32[]{:S(2)}) copy-start(bf16[2048,1024]{1,0:T(8,128)(2,1)} %get-tuple-element.37) | copy-start | bytes 12582916
  224.6 2.0 copy-start.1
  224.6 2.7 %copy-start.3 = (f32[1,1024]{1,0:T(1,128)S(1)}, f32[1,1024]{1,0:T(1,128)}, u32[]{:S(2)}) copy-start(f32[1,1024]{1,0:T(1,128)} %get-tuple-element.28) | copy-start | bytes 12292
  224.6 3.3 %copy-start.2 = (f32[1,1024]{1,0:T(1,128)S(1)}, f32[1,1024]{1,0:T(1,128)}, u32[]{:S(2)}) copy-start(f32[1,1024]{1,0:T(1,128)} %get-tuple-element.29) | copy-start | bytes 12292
